TPU v7x, 32 devices: a whole 2x2x4 slice. The times are simulated.
32 devices in a mesh: section: 2 (over x), dp: 16 (over z, y, core).
Axes of the slice: x: 2, y: 2, z: 4, core: 2. Of those that a mesh axis runs over, the one named last changes fastest.
Arguments:
- activations: bfloat16 [4, 256, 4608], P('section', 'dp'), may hold values from -6 to 6
- section_sources: int32 [4], replicated, may hold values from 0 to 3, as said below
- accumulators: float32 [256, 4, 4608], P('dp', 'section'), may hold values from -6 to 6
- block_sources: int32 [256], replicated, may hold values from 0 to 255, as said below
- loss_terms: float32 [2, 16], P('section', 'dp'), may hold values from 0.35 to 6
- pre_gain: float32 [2, 4608], P('section'), may hold values from 0.1 to 1.9
- query_weight: bfloat16 [2, 4608, 2048], P('section', None, 'dp'), may hold values from -0.09375 to 0.09375
- keyval_weight: bfloat16 [2, 4608, 2048], P('section', None, 'dp'), may hold values from -0.09375 to 0.09375
- output_weight: bfloat16 [2, 2048, 4608], P('section', 'dp'), may hold values from -0.125 to 0.125
- post_gain: float32 [2, 4608], P('section'), may hold values from 0.1 to 1.9
Outputs:
- new_activations: bfloat16 [4, 256, 4608], P('section', 'dp')
- new_accumulators: float32 [256, 4, 4608], P('dp', 'section')
- check_out: bfloat16 [2, 256, 4608], P('section', 'dp')
Inputs may be any that keep to these rules, and one draw needn't show every extreme that they name: `section_sources`: A permutation; each old section's micro-batches fill 1 slots of each new section. `block_sources`: A permutation; each old data index's blocks fill 1 block of each new data index.
All inputs are finite; a program needn't handle non-finite values.
Results may differ from a plain program's by a relative error of at most 0.014.
Values may be sent and summed in bfloat16 or wider, within the bound.
A program may use at most 64 MiB of HBM per device.

v0:
```python
import jax
import jax.numpy as jnp
from jax import lax
from jax.sharding import PartitionSpec as P

D = 4608


def partner(value, axis, stride):
    mask = 2**stride
    pairs = [(source, source ^ mask) for source in range(lax.axis_size(axis))]
    return lax.ppermute(value, axis, pairs)


def rms_norm(values, gain):
    meansq = jnp.mean(values * values, axis=-1, keepdims=True)
    return values * lax.rsqrt(meansq + 1e-06) * gain


def rotary(values, positions):
    width = values.shape[-1]
    middle = width // 2
    counter = jnp.arange(middle, dtype=jnp.float32)
    freqs = 10000.0 ** (-2.0 * counter / width)
    angles = positions.astype(jnp.float32)[:, None] * freqs[None, :]
    cosine = jnp.cos(angles)
    sine = jnp.sin(angles)
    first = values[..., :middle]
    second = values[..., middle:]
    return jnp.concatenate(
        [first * cosine - second * sine, second * cosine + first * sine], axis=-1
    )


def plan_routes(sources, own_index, groups, per_group):
    per_peer = per_group // groups
    table = sources.reshape(groups, per_group)
    owners = table // per_group
    places = table % per_group
    slot_ids = jnp.arange(per_group, dtype=jnp.int32)
    sort_keys = jnp.where(owners == own_index, slot_ids[None, :], slot_ids[None, :] + per_group)
    ranking = jnp.argsort(sort_keys, axis=1)[:, :per_peer]
    send_index = jnp.take_along_axis(places, ranking, axis=1).reshape(-1)
    my_owners = lax.dynamic_slice_in_dim(owners, own_index, 1, 0)[0]
    earlier = (my_owners[None, :] == my_owners[:, None]) & (slot_ids[None, :] < slot_ids[:, None])
    earlier_count = jnp.sum(earlier.astype(jnp.int32), axis=1)
    recv_index = my_owners * per_peer + earlier_count
    return (send_index, recv_index)


def on_device(
    activations,
    section_sources,
    accumulators,
    block_sources,
    loss_terms,
    pre_gain,
    query_weight,
    keyval_weight,
    output_weight,
    post_gain,
):
    section_index = lax.axis_index("section")
    mb_local = activations.shape[0]
    gathered = lax.all_gather(activations, "section", axis=0, tiled=True)
    my_slots = lax.dynamic_slice_in_dim(section_sources, section_index * mb_local, mb_local)
    moved = jnp.take(gathered, my_slots, axis=0)
    data_ranks = lax.axis_size("dp")
    data_index = lax.axis_index("dp")
    blk_local = accumulators.shape[0]
    per_peer = blk_local // data_ranks
    block_send, block_recv = plan_routes(block_sources, data_index, data_ranks, blk_local)
    outgoing_blocks = jnp.take(accumulators, block_send, axis=0)
    term_rows = jnp.broadcast_to(loss_terms, (blk_local, 1))
    incoming_blocks, incoming_terms = (
        lax.all_to_all(
            outgoing_blocks.astype(jnp.bfloat16), "dp", split_axis=0, concat_axis=0, tiled=True
        ).astype(outgoing_blocks.dtype),
        lax.all_to_all(
            term_rows.astype(jnp.bfloat16), "dp", split_axis=0, concat_axis=0, tiled=True
        ).astype(term_rows.dtype),
    )
    scale_sum = jnp.sum(incoming_terms[::per_peer, 0])
    factor = data_ranks / scale_sum
    new_accumulators = jnp.take(incoming_blocks, block_recv, axis=0) * factor
    checked = moved[0]
    head_size = query_weight.shape[2]
    is_even = data_index % 2 == 0
    w_query = query_weight[0]
    w_keyval = keyval_weight[0]
    gain_pre = pre_gain[0]
    block_rows = lax.all_gather(checked, "dp", axis=0, tiled=True)
    row_count = block_rows.shape[0]
    positions = jnp.arange(row_count, dtype=jnp.int32)
    normed = rms_norm(block_rows.astype(jnp.float32), gain_pre).astype(jnp.bfloat16)
    queries = jnp.dot(normed, w_query, preferred_element_type=jnp.float32)
    own_proj = jnp.dot(normed, w_keyval, preferred_element_type=jnp.float32)
    queries = rotary(queries, positions)
    own_proj = jnp.where(is_even, rotary(own_proj, positions), own_proj)
    projected = jnp.concatenate([queries, own_proj], axis=1).astype(jnp.bfloat16)
    queries = projected[:, :head_size]
    own_kv = projected[:, head_size:]
    partner_kv = partner(own_kv, "dp", 0)
    key_rows = jnp.where(is_even, own_kv, partner_kv)
    value_rows = jnp.where(is_even, partner_kv, own_kv)
    length = projected.shape[0]
    positions = jnp.arange(length, dtype=jnp.int32)
    scale_factor = (D / data_ranks) ** (-0.5)
    scores = (
        lax.dot_general(
            queries, key_rows, (((1,), (1,)), ((), ())), preferred_element_type=jnp.float32
        )
        * scale_factor
    )
    capped = 50.0 * jnp.tanh(scores / 50.0)
    causal = positions[None, :] <= positions[:, None]
    expd = jnp.where(causal, jnp.exp(capped), 0.0)
    denominator = jnp.sum(expd, axis=-1, keepdims=True)
    probs = expd.astype(jnp.bfloat16)
    numer = jnp.dot(probs, value_rows, preferred_element_type=jnp.float32)
    attended = (numer / denominator).astype(jnp.bfloat16)
    w_output = output_weight[0]
    summed = lax.psum_scatter(
        jnp.dot(attended, w_output, preferred_element_type=jnp.float32).astype(jnp.bfloat16),
        "dp",
        scatter_dimension=0,
        tiled=True,
    ).astype(jnp.float32)
    check_out = (checked.astype(jnp.float32) + rms_norm(summed, post_gain[0])).astype(jnp.bfloat16)
    return (moved, new_accumulators, check_out[None, :, :])


def solution(mesh):
    placed = (
        P("section", "dp", None),
        P(),
        P("dp", "section", None),
        P(),
        P("section", "dp"),
        P("section", None),
        P("section", None, "dp"),
        P("section", None, "dp"),
        P("section", "dp", None),
        P("section", None),
    )
    return jax.shard_map(
        on_device,
        mesh=mesh,
        in_specs=placed,
        out_specs=(P("section", "dp", None), P("dp", "section", None), P("section", "dp", None)),
        check_vma=False,
    )
```

profile of v0, /device:TPU:0, one launch (start us, length us, event | category | flops | bytes accessed | tf_op | source)
XLA Modules:
  0.0 145.7 jit_solution(12692090813205101284)
XLA Ops:
  7.2 0.0 copy-start
  7.2 0.0 copy-start.6
  7.2 0.0 copy-start.4
  7.2 0.0 all-gather.3.cloned.1.call-start
  7.3 0.8 compare_and_fusion.2
  8.1 10.9 %all_gather.6 = bf16[4,16,4608]{2,1,0:T(8,128)(2,1)S(1)} all-gather(bf16[2,16,4608]{2,1,0:T(8,128)(2,1)} %param.12), channel_id=1, replica_groups=mesh['section'=2,'dp'=16] {'section'}, dimensions={0}, use_global_device_ids=true | all-gather | bytes 884736 | tf_op jit(solution)/shard_map/all_gather | solution.py:65
  19.0 0.6 gather_fusion
  19.6 0.1 broadcast_select_fusion
  19.7 0.0 copy-start.2
  19.7 0.7 slice.38
  20.4 0.0 all-gather.3.cloned.1.call-update
  21.1 0.6 broadcast_in_dim.70
  21.7 6.1 %all-to-all-start.1 = ((bf16[16,1,1]{2,1,0:T(2,128)(2,1)}), bf16[16,1,1]{2,1,0:T(2,128)(2,1)S(1)}, u32[]{:S(2)}, u32[]{:S(2)}) async-start(bf16[16,1,1]{2,1,0:T(2,128)(2,1)} %broadcast_in_dim.70), calls=%async_computation.1 | async-start | bytes 16384 | tf_op jit(solution)/shard_map/all_to_all | solution.py:79
  27.8 0.0 reduce-scatter.2.cloned.1.call-start
  27.9 0.0 copy-done.6
  27.9 0.1 reshape.81
  28.0 0.1 copy.18
  28.1 0.0 copy-done.4
  28.1 0.7 sort.17
  28.9 35.5 %all-gather.3.cloned.1.call-done = bf16[1,256,4608]{2,1,0:T(8,128)(2,1)} async-done(((bf16[1,16,4608]{2,1,0:T(8,128)(2,1)}), bf16[1,256,4608]{2,1,0:T(8,128)(2,1)}) %all-gather.3.cloned.1.call-update) | async-done | bytes 2359312 | tf_op jit(solution)/shard_map/all_gather | solution.py:92
  64.4 0.0 copy-start.1
  64.4 2.4 %fusion = f32[256]{0:T(256)S(1)} fusion(bf16[1,256,4608]{2,1,0:T(8,128)(2,1)} %all-gather.3.cloned.1.call-done), kind=kLoop, calls=%fused_computation.7 | loop fusion | flops 3538688 | bytes 2360320 | tf_op jit(solution)/shard_map/reduce_sum | solution.py:16
  66.8 0.0 copy-done.1
  66.8 0.0 copy-start.7
  66.8 2.4 %fusion.4 = f32[256,128]{0,1:T(8,128)S(1)} fusion(bf16[1,4608,128]{2,1,0:T(8,128)(2,1)} %param.19, bf16[1,256,4608]{2,1,0:T(8,128)(2,1)S(1)} %copy-done.1, f32[4608]{0:T(1024)S(1)} %reduce.1, f32[256]{0:T(256)S(1)} %add_rsqrt_fusion), kind=kOutput, calls=%fused_computation.11 | convolution fusion | flops 306708480 | bytes 3689472 | tf_op jit(solution)/shard_map/dot_general | solution.py:97
  69.2 0.3 fusion.35
  69.5 0.3 collective-permute-start
  69.8 0.0 copy-done.7
  69.8 1.1 fusion.6
  70.9 0.3 fusion.32
  71.2 0.0 collective-permute-done
  71.3 0.3 fusion.52
  71.5 0.0 copy-done
  71.6 2.4 %convolution_convert_fusion = bf16[256,4608]{1,0:T(8,128)(2,1)} fusion(bf16[1,128,4608]{2,1,0:T(8,128)(2,1)S(1)} %copy-done, bf16[256,256]{0,1:T(8,128)(2,1)S(1)} %get-tuple-element.20, f32[256]{0:T(256)S(1)} %get-tuple-element.19, bf16[256,128]{0,1:T(8,128)(2,1)S(1)} %collective-permute-done, bf16[256,128]{0,1:T(8,128)(2,1)S(1)} %fusion.20, pred[]{:T(512)S(6)} %eq.31), kind=kOutput, calls=%fused_computation.4 | convolution fusion | flops 320045056 | bytes 3802113 | tf_op jit(solution)/shard_map/dot_general | solution.py:124
  74.0 0.0 copy-start.3
  74.0 0.0 copy-start.5
  74.0 0.0 reduce-scatter.2.cloned.1.call-update
  74.0 0.7 gather_fusion.1
  74.7 0.3 copy-done.3
  75.0 1.2 gather_fusion.2
  76.2 1.0 select_convert_fusion
  77.2 0.0 copy-done.5
  77.3 0.0 all-to-all-done.1
  77.3 3.6 %all-to-all-start = ((bf16[16,2,4608]{2,1,0:T(2,128)(2,1)}), bf16[16,2,4608]{2,1,0:T(2,128)(2,1)S(1)}, u32[]{:S(2)}, u32[]{:S(2)}) async-start(bf16[16,2,4608]{2,1,0:T(2,128)(2,1)} %select_convert_fusion), calls=%async_computation | async-start | bytes 589824 | tf_op jit(solution)/shard_map/all_to_all | solution.py:76
  80.9 0.2 convert_reduce_fusion
  81.1 0.1 copy.19
  81.2 0.6 convert_reduce_fusion.1
  82.5 8.9 %all-to-all-done = bf16[16,2,4608]{2,1,0:T(2,128)(2,1)S(1)} async-done(((bf16[16,2,4608]{2,1,0:T(2,128)(2,1)}), bf16[16,2,4608]{2,1,0:T(2,128)(2,1)S(1)}, u32[]{:S(2)}, u32[]{:S(2)}) %all-to-all-start) | async-done | bytes 294944 | tf_op jit(solution)/shard_map/all_to_all | solution.py:76
  91.4 0.2 convert_element_type.71
  91.6 1.2 gather_fusion.3
  92.8 1.1 select_multiply_fusion
  93.9 42.2 %reduce-scatter.2.cloned.1.call-done = bf16[16,4608]{1,0:T(8,128)(2,1)} async-done(((bf16[256,4608]{1,0:T(8,128)(2,1)}), bf16[16,4608]{1,0:T(8,128)(2,1)}) %reduce-scatter.2.cloned.1.call-update) | async-done | bytes 147472 | tf_op jit(solution)/shard_map/reduce_scatter | solution.py:123
  136.1 1.1 fusion.15
  137.1 0.0 copy-done.2
  137.1 1.7 %fusion.19 = bf16[1,16,4608]{2,1,0:T(8,128)(2,1)} fusion(bf16[16,4608]{1,0:T(8,128)(2,1)} %reduce-scatter.2.cloned.1.call-done, f32[4608]{0:T(1024)S(1)} %reduce.2, f32[16]{0:T(128)S(1)} %add_rsqrt_fusion.1, bf16[2,16,4608]{2,1,0:T(8,128)(2,1)S(1)} %broadcast_select_fusion), kind=kLoop, calls=%fused_computation.32 | loop fusion | flops 442368 | bytes 460864 | tf_op jit(solution)/shard_map/broadcast_in_dim | solution.py:130
  (20 shorter events, 0.2 us)
Async XLA Ops:
  7.2 64.4 %copy-start = (bf16[1,128,4608]{2,1,0:T(8,128)(2,1)S(1)}, bf16[1,128,4608]{2,1,0:T(8,128)(2,1)}, u32[]{:S(2)}) copy-start(bf16[1,128,4608]{2,1,0:T(8,128)(2,1)} %param.20) | copy-start | bytes 3538948
  7.2 20.7 %copy-start.6 = (s32[256]{0:T(256)S(1)}, s32[256]{0:T(256)}, u32[]{:S(2)}) copy-start(s32[256]{0:T(256)} %param.15) | copy-start | bytes 3076
  7.2 20.9 %copy-start.4 = (f32[1,4608]{1,0:T(1,128)S(1)}, f32[1,4608]{1,0:T(1,128)}, u32[]{:S(2)}) copy-start(f32[1,4608]{1,0:T(1,128)} %param.17) | copy-start | bytes 55300
  7.2 57.2 %all-gather.3.cloned.1.call-start = ((), (), s32[]{:S(2)}) async-start(), calls=%async_computation.4 | async-start | bytes 2506752 | tf_op jit(solution)/shard_map/all_gather | solution.py:92
  19.7 117.5 %copy-start.2 = (bf16[2,16,4608]{2,1,0:T(8,128)(2,1)}, bf16[2,16,4608]{2,1,0:T(8,128)(2,1)S(1)}, u32[]{:S(2)}) copy-start(bf16[2,16,4608]{2,1,0:T(8,128)(2,1)S(1)} %broadcast_select_fusion) | copy-start | bytes 884740
  21.7 55.6 %all-to-all-start.1 = ((bf16[16,1,1]{2,1,0:T(2,128)(2,1)}), bf16[16,1,1]{2,1,0:T(2,128)(2,1)S(1)}, u32[]{:S(2)}, u32[]{:S(2)}) async-start(bf16[16,1,1]{2,1,0:T(2,128)(2,1)} %broadcast_in_dim.70), calls=%async_computation.1 | async-start | bytes 16384 | tf_op jit(solution)/shard_map/all_to_all | solution.py:79
  27.8 108.3 %reduce-scatter.2.cloned.1.call-start = ((), (), s32[]{:S(2)}) async-start(), calls=%async_computation.3 | async-start | bytes 2506752 | tf_op jit(solution)/shard_map/reduce_scatter | solution.py:123
  64.4 2.4 %copy-start.1 = (bf16[1,256,4608]{2,1,0:T(8,128)(2,1)S(1)}, bf16[1,256,4608]{2,1,0:T(8,128)(2,1)}, u32[]{:S(2)}) copy-start(bf16[1,256,4608]{2,1,0:T(8,128)(2,1)} %all-gather.3.cloned.1.call-done) | copy-start | bytes 7077892
  66.8 3.1 %copy-start.7 = (bf16[1,4608,128]{2,1,0:T(8,128)(2,1)S(1)}, bf16[1,4608,128]{2,1,0:T(8,128)(2,1)}, u32[]{:S(2)}) copy-start(bf16[1,4608,128]{2,1,0:T(8,128)(2,1)} %param.18) | copy-start | bytes 3538948
  69.5 1.7 %collective-permute-start = (bf16[256,128]{0,1:T(8,128)(2,1)S(1)}, bf16[256,128]{0,1:T(8,128)(2,1)S(1)}, u32[]{:S(2)}, u32[]{:S(2)}) collective-permute-start(bf16[256,128]{0,1:T(8,128)(2,1)S(1)} %fusion.20), channel_id=1, source_target_pairs={{0,1},{1,0},{2,3},{3,2},{4,5},{5,4},{6,7},{7,6},{8,9},{9,8},{10,11... | collective-permute-start | bytes 196616 | tf_op jit(solution)/shard_map/ppermute | solution.py:12
  74.0 1.1 copy-start.3
  74.0 3.3 %copy-start.5 = (f32[1,4608]{1,0:T(1,128)S(1)}, f32[1,4608]{1,0:T(1,128)}, u32[]{:S(2)}) copy-start(f32[1,4608]{1,0:T(1,128)} %param.21) | copy-start | bytes 55300
  77.3 14.1 %all-to-all-start = ((bf16[16,2,4608]{2,1,0:T(2,128)(2,1)}), bf16[16,2,4608]{2,1,0:T(2,128)(2,1)S(1)}, u32[]{:S(2)}, u32[]{:S(2)}) async-start(bf16[16,2,4608]{2,1,0:T(2,128)(2,1)} %select_convert_fusion), calls=%async_computation | async-start | bytes 589824 | tf_op jit(solution)/shard_map/all_to_all | solution.py:76
Sparse Core Ops, SparseCore 0:
  20.5 43.7 all-gather.2
  74.1 61.9 reduce-scatter.1
where the time goes:
time: 146 us
  waiting for transfers between devices  86.6 us (59%)
  between operations  15.7 us (11%)
  blocking collectives  10.9 us (7%)
  other arithmetic  10.8 us (7%)
  starting transfers between devices  10.1 us (7%)
  matrix products  6.18 us (4%)
  local copies, waits for them, and re-layouts  5.5 us (4%)
    reduce_scatter x1, waiting for transfers between devices, on_device(): lax.psum_scatter(jnp.dot(attended, w_output, preferred_element_type=jnp.f...  42.2 us
    all_gather x1, waiting for transfers between devices, on_device(): block_rows = lax.all_gather(checked, 'dp', axis=0, tiled=True)  35.5 us
    all_gather x1, blocking collectives, on_device(): gathered = lax.all_gather(activations, 'section', axis=0, tiled=True)  10.9 us
    all_to_all x1, waiting for transfers between devices, on_device(): lax.all_to_all(outgoing_blocks.astype(jnp.bfloat16), 'dp', split_axis=0,...  8.9 us
    all_to_all x1, starting transfers between devices, on_device(): lax.all_to_all(term_rows.astype(jnp.bfloat16), 'dp', split_axis=0, concat...  6.13 us
    all_to_all x1, starting transfers between devices, on_device(): lax.all_to_all(outgoing_blocks.astype(jnp.bfloat16), 'dp', split_axis=0,...  3.55 us
    reduce_sum x2, other arithmetic, rms_norm(): meansq = jnp.mean(values * values, axis=-1, keepdims=True)  3.42 us
  transfers between devices with their start and end apart: 5, of which 3 were waited for; matrix products, arithmetic and copies ran while one was open for 12% of the time, Pallas kernels for 0%

commit v1 on v0

v1 whole, which is shorter than its diff:
```python
import functools

import jax
import jax.numpy as jnp
import numpy as np
from jax import lax
from jax.experimental import pallas as pl
from jax.experimental.pallas import tpu as pltpu
from jax.sharding import PartitionSpec as P

LANES = 128
CHUNKS = 4
F32 = jnp.float32
BF16 = jnp.bfloat16


def routes(sources, own, groups, per_group):
    per_peer = per_group // groups
    table = sources.reshape(groups, per_group)
    owners = table // per_group
    places = table % per_group
    mine = owners == own
    my_owners = lax.dynamic_slice_in_dim(owners, own, 1, 0)[0]
    if per_peer == 1:
        send = jnp.sum(jnp.where(mine, places, 0), axis=1)
        return send, my_owners
    rank = jnp.cumsum(mine.astype(jnp.int32), axis=1) - 1
    picked = mine[:, None, :] & (rank[:, None, :] == jnp.arange(per_peer)[None, :, None])
    send = jnp.sum(jnp.where(picked, places[:, None, :], 0), axis=2).reshape(-1)
    ids = jnp.arange(per_group)
    earlier = (my_owners[None, :] == my_owners[:, None]) & (ids[None, :] < ids[:, None])
    return send, my_owners * per_peer + jnp.sum(earlier.astype(jnp.int32), axis=1)


def rotary_tables(length, width):
    half = width // 2
    freqs = np.float32(10000.0) ** (np.float32(-2.0) * np.arange(half, dtype=np.float32) / np.float32(width))
    angles = np.arange(length, dtype=np.float32)[:, None] * freqs.astype(np.float32)[None, :]
    cosine, sine = np.cos(angles.astype(np.float64)), np.sin(angles.astype(np.float64))
    return np.stack(
        [np.concatenate([cosine, cosine], 1), np.concatenate([-sine, sine], 1)]
    ).astype(np.float32)


def kernel(
    dims,
    act_send, act_recv, blk_send, blk_recv, loss,
    act_hbm, acc_hbm, pre_hbm, wq_hbm, wkv_hbm, wo_hbm, post_hbm, rot_hbm,
    moved_hbm, newacc_hbm, check_hbm,
    act, acc, pre, post, rot, w, wo,
    stage, actrecv, moved, sacc, racc, accout,
    gath, qkv, part, pair_in, ring_in, ring_out, outbuf,
    load_sem, store_sem, act_sem, w_sem, blk_sem, ag_sem, own_sem, fwd_sem, pair_sem, ring_sem,
):
    n_sec, n_dp = dims
    mb, toks, d = act.shape
    blk, brows, _ = acc.shape
    act_pp, blk_pp = mb // n_sec, blk // n_dp
    chips = n_dp // 2
    far = chips // 2
    kd = d // CHUNKS
    length = n_dp * toks
    hd = wq_hbm.shape[2]
    sec, me = lax.axis_index("section"), lax.axis_index("dp")
    core, chip = me % 2, me // 2
    side, rung = chip % 2, chip // 2
    pos = rung * (1 - side) + (chips - 1 - rung) * side

    def chip_at(p):
        q = (p + 2 * chips) % chips
        s = q // (chips // 2)
        return 2 * (q * (1 - s) + (chips - 1 - q) * s) + s

    def device(p):
        return {"dp": 2 * chip_at(p) + core}

    partner = {"dp": me + 1 - 2 * core}

    def remote(src, dst, sems, dev):
        return pltpu.make_async_remote_copy(
            src_ref=src, dst_ref=dst, send_sem=sems.at[0], recv_sem=sems.at[1],
            device_id=dev, device_id_type=pl.DeviceIdType.MESH,
        )

    barrier = pltpu.get_barrier_semaphore()
    for o in range(1, n_sec):
        pl.semaphore_signal(barrier, inc=1, device_id={"section": (sec + o) % n_sec},
                            device_id_type=pl.DeviceIdType.MESH)
    for o in range(1, n_dp):
        pl.semaphore_signal(barrier, inc=1, device_id={"dp": (me + o) % n_dp},
                            device_id_type=pl.DeviceIdType.MESH)

    kv_cols = pl.ds(pl.multiple_of(hd + core * hd, LANES), hd)
    loads = [
        pltpu.make_async_copy(src, dst, load_sem.at[i])
        for i, (src, dst) in enumerate([
            (act_hbm, act), (wkv_hbm.at[0], w.at[:, kv_cols]), (pre_hbm, pre), (acc_hbm, acc),
            (wq_hbm.at[0], w.at[:, pl.ds(0, hd)]), (rot_hbm, rot), (wo_hbm.at[0], wo), (post_hbm, post),
        ])
    ]
    for load in loads:
        load.start()

    loads[0].wait()
    for q in range(n_sec):
        for r in range(act_pp):
            stage[q, r] = act[act_send[q * act_pp + r]]
    pl.semaphore_wait(barrier, n_sec - 1 + n_dp - 1)
    act_copies = []
    for o in range(1, n_sec):
        q = (sec + o) % n_sec
        copy = remote(stage.at[q], actrecv.at[sec], act_sem.at[o - 1], {"section": q})
        copy.start()
        act_copies.append(copy)
    actrecv[sec] = stage[sec]

    loads[1].wait()
    kv_copy = remote(w.at[:, kv_cols], w.at[:, kv_cols], w_sem, partner)
    kv_copy.start()

    loads[3].wait()
    term = jnp.full((brows, LANES), loss[0, 0], F32)
    high = term.astype(BF16).astype(F32)
    row = lax.broadcasted_iota(jnp.int32, (brows, LANES), 0)
    tail = jnp.where(row == 0, high, jnp.where(row == 1, term - high, 0.0)).astype(BF16)

    def pack(p, carry):
        for r in range(blk_pp):
            sacc[p, r, :, pl.ds(0, d)] = acc[blk_send[p * blk_pp + r]].astype(BF16)
            sacc[p, r, :, pl.ds(d, LANES)] = tail
        return carry

    lax.fori_loop(0, n_dp, pack, 0)
    racc[me] = sacc[me]

    loads[2].wait()
    for copy in act_copies:
        copy.wait_recv()
    for j in range(mb):
        src = act_recv[j]
        moved[j] = actrecv[src // act_pp, src % act_pp] if act_pp > 1 else actrecv[src, 0]
    checked = moved[0].astype(F32)
    normed = checked * lax.rsqrt(jnp.mean(checked * checked, axis=-1, keepdims=True) + 1e-06)
    normed = (normed * pre[...]).astype(BF16)
    for k in range(CHUNKS):
        gath[k, me] = normed[:, k * kd:(k + 1) * kd]
    stores = [pltpu.make_async_copy(moved, moved_hbm, store_sem.at[0])]
    stores[0].start()

    def hops(way, k):
        return far if (k < CHUNKS // 2) == (way == 0) else far - 1

    step_of = (1, -1)
    sent = []

    def gather_copy(way, hop, k, source):
        block = gath.at[k, source]
        return remote(block, block, ag_sem.at[way, hop - 1, k], device(pos + step_of[way]))

    def pass_on(source, k, sems):
        block = gath.at[k, source]
        copy = remote(block, block, sems, partner)
        copy.start()
        sent.append(copy)

    for k in range(CHUNKS):
        for way in range(2):
            copy = gather_copy(way, 1, k, me)
            copy.start()
            sent.append(copy)
    for k in range(CHUNKS):
        pass_on(me, k, own_sem.at[k])
    for hop in range(1, far + 1):
        for k in range(CHUNKS):
            for way in range(2):
                if hop > hops(way, k):
                    continue
                source = 2 * chip_at(pos - step_of[way] * hop) + core
                gather_copy(way, hop, k, source).wait_recv()
                if hop < hops(way, k):
                    copy = gather_copy(way, hop + 1, k, source)
                    copy.start()
                    sent.append(copy)
                pass_on(source, k, fwd_sem.at[way, hop - 1, k])

    blk_copies = []
    for o in range(1, n_dp):
        peer = (me + o) % n_dp
        copy = remote(sacc.at[peer], racc.at[me], blk_sem.at[o - 1], {"dp": peer})
        copy.start()
        blk_copies.append(copy)

    kv_copy.wait_recv()
    loads[4].wait()
    other = me + 1 - 2 * core
    for k in range(CHUNKS):
        remote(gath.at[k, other], gath.at[k, other], own_sem.at[k], partner).wait_recv()
    for hop in range(1, far + 1):
        for k in range(CHUNKS):
            for way in range(2):
                if hop <= hops(way, k):
                    source = 2 * chip_at(pos - step_of[way] * hop) + 1 - core
                    block = gath.at[k, source]
                    remote(block, block, fwd_sem.at[way, hop - 1, k], partner).wait_recv()

    qkv[...] = jnp.zeros_like(qkv)

    def project(k, carry):
        rows = gath[k].reshape(length, kd)
        cols = w[pl.ds(pl.multiple_of(k * kd, LANES), kd), :]
        qkv[...] += jnp.dot(rows, cols, preferred_element_type=F32)
        return carry

    lax.fori_loop(0, CHUNKS, project, 0)
    loads[5].wait()
    cosine, sine = rot[0], rot[1]

    def turned(v):
        return (v * cosine + pltpu.roll(v, hd // 2, 1) * sine).astype(BF16)

    queries = turned(qkv[:, 0:hd])
    keys = turned(qkv[:, hd:2 * hd])
    values = qkv[:, 2 * hd:3 * hd].astype(BF16)
    scores = lax.dot_general(queries, keys, (((1,), (1,)), ((), ())), preferred_element_type=F32)
    scores = scores * ((d / n_dp) ** (-0.5) / 50.0)
    at_query = lax.broadcasted_iota(jnp.int32, scores.shape, 0)
    at_key = lax.broadcasted_iota(jnp.int32, scores.shape, 1)
    expd = jnp.where(at_key <= at_query, jnp.exp(50.0 * jnp.tanh(scores)), 0.0)
    denominator = jnp.sum(expd, axis=-1, keepdims=True)
    numer = jnp.dot(expd.astype(BF16), values, preferred_element_type=F32)
    attended = (numer / denominator).astype(BF16)

    loads[6].wait()
    pair_copies = []
    for k in range(CHUNKS):
        terms = jnp.dot(attended, wo[:, k * kd:(k + 1) * kd], preferred_element_type=F32).astype(BF16)
        part[k] = terms.reshape(chips, 2, toks, kd)
        copy = remote(part.at[k, :, 1 - core], pair_in.at[k], pair_sem.at[k], partner)
        copy.start()
        pair_copies.append(copy)

    def own_terms(k, p):
        target = chip_at(p)
        return part[k, target, core].astype(F32) + pair_in[k, target].astype(F32)

    def ring_copy(way, step, k):
        return remote(ring_out.at[way, step - 1, k], ring_in.at[way, step - 1, k],
                      ring_sem.at[way, step - 1, k], device(pos + step_of[way]))

    for k in range(CHUNKS):
        pair_copies[k].wait_recv()
        for way in range(2):
            ring_out[way, 0, k] = own_terms(k, pos + step_of[way] * hops(way, k)).astype(BF16)
            copy = ring_copy(way, 1, k)
            copy.start()
            sent.append(copy)
    for step in range(1, far):
        for k in range(CHUNKS):
            for way in range(2):
                left = hops(way, k) - step
                if left < 1:
                    continue
                ring_copy(way, step, k).wait_recv()
                total = own_terms(k, pos + step_of[way] * left) + ring_in[way, step - 1, k].astype(F32)
                ring_out[way, step, k] = total.astype(BF16)
                copy = ring_copy(way, step + 1, k)
                copy.start()
                sent.append(copy)

    for copy in blk_copies:
        copy.wait_recv()
    scale_sum = jnp.sum(jnp.sum(racc[:, 0, :, pl.ds(d, LANES)].astype(F32), axis=0), axis=0, keepdims=True)
    factor = (n_dp / scale_sum)[:, 0:1]

    def unpack(b, carry):
        src = blk_recv[b]
        if blk_pp > 1:
            block = racc[src // blk_pp, src % blk_pp, :, pl.ds(0, d)]
        else:
            block = racc[src, 0, :, pl.ds(0, d)]
        accout[b] = block.astype(F32) * factor
        return carry

    lax.fori_loop(0, blk, unpack, 0)
    stores.append(pltpu.make_async_copy(accout, newacc_hbm, store_sem.at[1]))
    stores[1].start()

    pieces = []
    for k in range(CHUNKS):
        total = own_terms(k, pos)
        for way in range(2):
            step = hops(way, k)
            ring_copy(way, step, k).wait_recv()
            total = total + ring_in[way, step - 1, k].astype(F32)
        pieces.append(total)
    loads[7].wait()
    square = sum(jnp.sum(t * t, axis=-1, keepdims=True) for t in pieces)
    scale = lax.rsqrt(square / d + 1e-06)
    for k in range(CHUNKS):
        cols = slice(k * kd, (k + 1) * kd)
        outbuf[0, :, cols] = (
            moved[0, :, cols].astype(F32) + pieces[k] * scale * post[:, cols]
        ).astype(BF16)
    stores.append(pltpu.make_async_copy(outbuf, check_hbm, store_sem.at[2]))
    stores[2].start()

    for copy in act_copies + [kv_copy] + sent + blk_copies + pair_copies:
        copy.wait_send()
    for store in stores:
        store.wait()


def make_on_device(n_sec, n_dp):
    def on_device(activations, section_sources, accumulators, block_sources, loss_terms,
                  pre_gain, query_weight, keyval_weight, output_weight, post_gain):
        mb, toks, d = activations.shape
        blk, brows, _ = accumulators.shape
        hd = query_weight.shape[2]
        chips, far, kd, length = n_dp // 2, n_dp // 4, d // CHUNKS, n_dp * toks
        act_send, act_recv = routes(section_sources, lax.axis_index("section"), n_sec, mb)
        blk_send, blk_recv = routes(block_sources, lax.axis_index("dp"), n_dp, blk)
        rot = jnp.asarray(rotary_tables(length, hd))
        smem = pl.BlockSpec(memory_space=pltpu.SMEM)
        anywhere = pl.BlockSpec(memory_space=pl.ANY)
        dma = pltpu.SemaphoreType.DMA
        act_pp, blk_pp = mb // n_sec, blk // n_dp

        return pl.pallas_call(
            functools.partial(kernel, (n_sec, n_dp)),
            out_shape=(
                jax.ShapeDtypeStruct(activations.shape, BF16),
                jax.ShapeDtypeStruct(accumulators.shape, F32),
                jax.ShapeDtypeStruct((1, toks, d), BF16),
            ),
            in_specs=[smem] * 5 + [anywhere] * 8,
            out_specs=(anywhere,) * 3,
            scratch_shapes=[
                pltpu.VMEM(activations.shape, BF16),
                pltpu.VMEM(accumulators.shape, F32),
                pltpu.VMEM((1, d), F32),
                pltpu.VMEM((1, d), F32),
                pltpu.VMEM(rot.shape, F32),
                pltpu.VMEM((d, 3 * hd), BF16),
                pltpu.VMEM((hd, d), BF16),
                pltpu.VMEM((n_sec, act_pp, toks, d), BF16),
                pltpu.VMEM((n_sec, act_pp, toks, d), BF16),
                pltpu.VMEM(activations.shape, BF16),
                pltpu.VMEM((n_dp, blk_pp, brows, d + LANES), BF16),
                pltpu.VMEM((n_dp, blk_pp, brows, d + LANES), BF16),
                pltpu.VMEM(accumulators.shape, F32),
                pltpu.VMEM((CHUNKS, n_dp, toks, kd), BF16),
                pltpu.VMEM((length, 3 * hd), F32),
                pltpu.VMEM((CHUNKS, chips, 2, toks, kd), BF16),
                pltpu.VMEM((CHUNKS, chips, toks, kd), BF16),
                pltpu.VMEM((2, far, CHUNKS, toks, kd), BF16),
                pltpu.VMEM((2, far, CHUNKS, toks, kd), BF16),
                pltpu.VMEM((1, toks, d), BF16),
                dma((8,)),
                dma((3,)),
                dma((n_sec - 1, 2)),
                dma((2,)),
                dma((n_dp - 1, 2)),
                dma((2, far, CHUNKS, 2)),
                dma((CHUNKS, 2)),
                dma((2, far, CHUNKS, 2)),
                dma((CHUNKS, 2)),
                dma((2, far, CHUNKS, 2)),
            ],
            compiler_params=pltpu.CompilerParams(
                collective_id=0, has_side_effects=True, vmem_limit_bytes=60 * 2**20
            ),
        )(act_send, act_recv, blk_send, blk_recv, loss_terms, activations, accumulators,
          pre_gain, query_weight, keyval_weight, output_weight, post_gain, rot)

    return on_device


def solution(mesh):
    placed = (
        P("section", "dp", None),
        P(),
        P("dp", "section", None),
        P(),
        P("section", "dp"),
        P("section", None),
        P("section", None, "dp"),
        P("section", None, "dp"),
        P("section", "dp", None),
        P("section", None),
    )
    return jax.shard_map(
        make_on_device(mesh.shape["section"], mesh.shape["dp"]),
        mesh=mesh,
        in_specs=placed,
        out_specs=(P("section", "dp", None), P("dp", "section", None), P("section", "dp", None)),
        check_vma=False,
    )
```

time: 146 us -> 61.9 us (0.42)
  waiting for transfers between devices: 86.6 us -> 0 us
  Pallas kernels: 0 us -> 52.1 us
  between operations: 15.7 us -> 1.3 us
  blocking collectives: 10.9 us -> 0 us
  starting transfers between devices: 10.1 us -> 0 us
  other arithmetic: 10.8 us -> 1.27 us
  matrix products: 6.18 us -> 0 us
    pallas_call x0 -> x1, Pallas kernels: none -> 52.1 us  [on_device(): pl.pallas_call(functools.partial(kernel, (n_sec, n_dp)), out_shape=(jax.S...]
    reduce_scatter x1 -> x0, waiting for transfers between devices: 42.2 us -> none  [on_device(): lax.psum_scatter(jnp.dot(attended, w_output, preferred_element_type=jnp.f...]
    all_gather x1 -> x0, waiting for transfers between devices: 35.5 us -> none  [on_device(): block_rows = lax.all_gather(checked, 'dp', axis=0, tiled=True)]
    all_gather x1 -> x0, blocking collectives: 10.9 us -> none  [on_device(): gathered = lax.all_gather(activations, 'section', axis=0, tiled=True)]
    all_to_all x2 -> x0, starting transfers between devices: 9.68 us -> none  [the longest x1 6.13 us: on_device(): lax.all_to_all(term_rows.astype(jnp.bfloat16), 'dp', split_axis=0, concat...]
    all_to_all x2 -> x0, waiting for transfers between devices: 8.9 us -> none  [the longest x1 8.9 us: on_device(): lax.all_to_all(outgoing_blocks.astype(jnp.bfloat16), 'dp', split_axis=0,...]
    dot_general x4 -> x0, matrix products: 6.18 us -> none  [the longest x1 2.42 us: on_device(): own_proj = jnp.dot(normed, w_keyval, preferred_element_type=jnp.float32)]
    unnamed x17 -> x5, local copies, waits for them, and re-layouts: 0.34 us -> 4.31 us
  transfers between devices with their start and end apart: 5 -> 0, of which waited for: 3 -> 0; matrix products, arithmetic and copies ran while one was open for 12% -> 0% of each run, Pallas kernels for 0% -> 0%
where the time goes in v1:
time: 61.9 us; the launch traced here: 61.6 us
  Pallas kernels  52.1 us (84%)
  local copies, waits for them, and re-layouts  6.91 us (11%)
  between operations  1.3 us (2%)
  other arithmetic  1.27 us (2%)
    pallas_call x1, Pallas kernels, on_device(): pl.pallas_call(functools.partial(kernel, (n_sec, n_dp)), out_shape=(jax.S...  52.1 us
    unnamed x5, local copies, waits for them, and re-layouts  4.31 us
    reshape x2, local copies, waits for them, and re-layouts, routes(): table = sources.reshape(groups, per_group)  1.49 us

profile of v1, /device:TPU:0, one launch (start us, length us, event | category | flops | bytes accessed | tf_op | source)
XLA Modules:
  0.0 61.6 jit_solution(7938903332794692525)
XLA Ops:
  1.3 0.7 %reshape.12 = s32[2,2]{1,0:T(2,128)S(1)} reshape(s32[4]{0:T(128)} %param.12) | data formatting | bytes 32 | tf_op jit(solution)/shard_map/reshape | solution.py:19
  2.0 0.6 %fusion.4 = (s32[2]{0:T(128)}, s32[2,2]{1,0:T(2,128)S(1)}) fusion(s32[]{:T(128)S(6)} %axis_index.23, s32[2,2]{1,0:T(2,128)S(1)} %reshape.12), kind=kLoop, calls=%fused_computation.16 | loop fusion | flops 86 | bytes 44 | tf_op jit(solution)/shard_map/reduce_sum | solution.py:25
  2.7 0.5 dynamic-slice_bitcast_fusion.1.act_recv
  3.2 0.8 %reshape.13 = s32[16,16]{1,0:T(8,128)S(1)} reshape(s32[256]{0:T(256)} %param.14) | data formatting | bytes 2048 | tf_op jit(solution)/shard_map/reshape | solution.py:19
  3.9 0.6 %add_select_fusion.1 = (s32[16,16]{1,0:T(8,128)S(1)}, s32[16]{0:T(128)}) fusion(s32[16,16]{1,0:T(8,128)S(1)} %reshape.13, s32[]{:T(128)S(6)} %axis_index.25), kind=kLoop, calls=%fused_computation.1 | loop fusion | flops 5616 | bytes 2116 | tf_op jit(solution)/shard_map/jit(floor_divide)/jit(_where)/select_n | solution.py:20
  4.6 0.6 dynamic-slice_bitcast_fusion.blk_recv
  5.2 52.1 %shard_map.130 = (bf16[2,16,4608]{2,1,0:T(8,128)(2,1)}, f32[16,2,4608]{2,1,0:T(2,128)}, bf16[1,16,4608]{2,1,0:T(8,128)(2,1)}) custom-call(s32[2]{0:T(128)} %get-tuple-element.3.act_send, s32[2]{0:T(128)} %dynamic-slice_bitcast_fusion.1.act_recv, s32[16]{0:T(128)} %get-tuple-element.6.blk_send, s32[16]{0:T(128)} %dynamic-slice_bitcast_fusion.blk_recv, ...), custom_call_target="tpu_custom_call" | custom-call | tf_op jit(solution)/shard_map/pallas_call | solution.py:328
  57.3 0.0 copy-start
  57.3 1.7 %copy.18 = bf16[2,16,4608]{2,1,0:T(8,128)(2,1)} copy(bf16[2,16,4608]{2,1,0:T(8,128)(2,1)} %get-tuple-element.10) | data formatting | bytes 589824
  59.0 1.9 %copy.19 = f32[16,2,4608]{2,1,0:T(2,128)} copy(f32[16,2,4608]{2,1,0:T(2,128)} %get-tuple-element.11) | data formatting | bytes 1179648
  61.0 0.0 copy-done
  61.0 0.7 %copy.20 = bf16[1,16,4608]{2,1,0:T(8,128)(2,1)} copy(bf16[1,16,4608]{2,1,0:T(8,128)(2,1)S(1)} %copy-done) | data formatting | bytes 294912
Async XLA Ops:
  57.3 3.7 %copy-start = (bf16[1,16,4608]{2,1,0:T(8,128)(2,1)S(1)}, bf16[1,16,4608]{2,1,0:T(8,128)(2,1)}, u32[]{:S(2)}) copy-start(bf16[1,16,4608]{2,1,0:T(8,128)(2,1)} %get-tuple-element.12) | copy-start | bytes 442372

commit v2 on v1

v2 whole, which is shorter than its diff:
```python
import functools

import jax
import jax.numpy as jnp
import numpy as np
from jax import lax
from jax.experimental import pallas as pl
from jax.experimental.pallas import tpu as pltpu
from jax.sharding import PartitionSpec as P

LANES = 128
VMEM_BYTES = 67043328
CHUNKS = 4
F32 = jnp.float32
BF16 = jnp.bfloat16


def pick(table, own, groups, per_group, peer, rank):
    def visit(j, carry):
        seen, found = carry
        source = table[peer * per_group + j]
        mine = (source // per_group == own).astype(jnp.int32)
        hit = mine * (seen == rank).astype(jnp.int32)
        return seen + mine, found + hit * (source % per_group)

    zero = jnp.int32(0)
    return lax.fori_loop(0, per_group, visit, (zero, zero), unroll=True)[1]


def origin(table, own, per_group, per_peer, entry):
    owner = table[own * per_group + entry] // per_group
    if per_peer == 1:
        return owner, 0

    def visit(j, seen):
        same = table[own * per_group + j] // per_group == owner
        return seen + same.astype(jnp.int32) * (j < entry).astype(jnp.int32)

    return owner, lax.fori_loop(0, per_group, visit, jnp.int32(0))


def rotary_tables(length, width):
    half = width // 2
    freqs = np.float32(10000.0) ** (np.float32(-2.0) * np.arange(half, dtype=np.float32) / np.float32(width))
    angles = np.arange(length, dtype=np.float32)[:, None] * freqs.astype(np.float32)[None, :]
    cosine, sine = np.cos(angles.astype(np.float64)), np.sin(angles.astype(np.float64))
    return np.stack(
        [np.concatenate([cosine, cosine], 1), np.concatenate([-sine, sine], 1)]
    ).astype(np.float32)


def kernel(
    dims,
    secs_hbm, blks_hbm, loss_hbm, act_hbm, acc_hbm, pre_hbm, wq_hbm, wkv_hbm, wo_hbm, post_hbm, rot_hbm,
    moved, accout, outbuf,
    secs, blks, loss, act, acc, pre, post, rot, w, wo,
    stage, actrecv, sacc, racc,
    gath, qkv, att, att_in, part, ring_in, ring_out,
    load_sem, act_sem, w_sem, wo_sem, blk_sem, ag_sem, own_sem, fwd_sem, att_sem, ring_sem,
):
    n_sec, n_dp = dims
    mb, toks, d = act.shape
    blk, brows, _ = acc.shape
    act_pp, blk_pp = mb // n_sec, blk // n_dp
    chips = n_dp // 2
    far = chips // 2
    kd = d // CHUNKS
    length = n_dp * toks
    hd = wq_hbm.shape[2]
    sec, me = lax.axis_index("section"), lax.axis_index("dp")
    core, chip = me % 2, me // 2
    side, rung = chip % 2, chip // 2
    pos = rung * (1 - side) + (chips - 1 - rung) * side

    def chip_at(p):
        q = (p + 2 * chips) % chips
        s = q // (chips // 2)
        return 2 * (q * (1 - s) + (chips - 1 - q) * s) + s

    def device(p):
        return {"dp": 2 * chip_at(p) + core}

    partner = {"dp": me + 1 - 2 * core}

    def remote(src, dst, sems, dev):
        return pltpu.make_async_remote_copy(
            src_ref=src, dst_ref=dst, send_sem=sems.at[0], recv_sem=sems.at[1],
            device_id=dev, device_id_type=pl.DeviceIdType.MESH,
        )

    barrier = pltpu.get_barrier_semaphore()
    for o in range(1, n_sec):
        pl.semaphore_signal(barrier, inc=1, device_id={"section": (sec + o) % n_sec},
                            device_id_type=pl.DeviceIdType.MESH)
    for o in range(1, n_dp):
        pl.semaphore_signal(barrier, inc=1, device_id={"dp": (me + o) % n_dp},
                            device_id_type=pl.DeviceIdType.MESH)

    kv_cols = pl.ds(pl.multiple_of(hd + core * hd, LANES), hd)
    q_cols = pl.ds(0, hd)
    wo_rows = pl.ds(pl.multiple_of(core * hd, LANES), hd)
    names = ("secs", "act", "pre", "wkv", "wo", "blks", "loss", "acc", "wq", "rot", "post")
    pairs = [
        (secs_hbm, secs), (act_hbm, act), (pre_hbm, pre), (wkv_hbm.at[0], w.at[:, kv_cols]),
        (wo_hbm.at[0], wo.at[wo_rows]), (blks_hbm, blks), (loss_hbm, loss), (acc_hbm, acc),
        (wq_hbm.at[0], w.at[:, q_cols]), (rot_hbm, rot), (post_hbm, post),
    ]
    loads = {
        name: pltpu.make_async_copy(src, dst, load_sem.at[i])
        for i, (name, (src, dst)) in enumerate(zip(names, pairs))
    }
    for name in names:
        loads[name].start()

    loads["secs"].wait()
    loads["act"].wait()
    for q in range(n_sec):
        for r in range(act_pp):
            block = act[pick(secs, sec, n_sec, mb, q, r)]
            for k in range(CHUNKS):
                stage[q, k, r] = block[:, k * kd:(k + 1) * kd]
    pl.semaphore_wait(barrier, n_sec - 1 + n_dp - 1)
    act_copies = [[] for _ in range(CHUNKS)]
    for k in range(CHUNKS):
        for o in range(1, n_sec):
            q = (sec + o) % n_sec
            copy = remote(stage.at[q, k], actrecv[k].at[sec], act_sem.at[o - 1, k], {"section": q})
            copy.start()
            act_copies[k].append(copy)
    for k in range(CHUNKS):
        actrecv[k][sec] = stage[sec, k]

    loads["wkv"].wait()
    kv_copy = remote(w.at[:, kv_cols], w.at[:, kv_cols], w_sem, partner)
    kv_copy.start()
    loads["wo"].wait()
    wo_copy = remote(wo.at[wo_rows], wo.at[wo_rows], wo_sem, partner)
    wo_copy.start()
    loads["pre"].wait()

    def hops(way, k):
        return far if (k < CHUNKS // 2) == (way == 0) else far - 1

    step_of = (1, -1)
    sent = []

    def width(k):
        return kd + LANES if k == CHUNKS - 1 else kd

    def block_of(k, source):
        return gath.at[k, source, :, pl.ds(0, width(k))]

    def gather_copy(way, hop, k, source):
        block = block_of(k, source)
        return remote(block, block, ag_sem.at[way, hop - 1, k], device(pos + step_of[way]))

    def hand_over(source, k, sems):
        block = block_of(k, source)
        return remote(block, block, sems, partner)

    def pass_on(source, k, sems):
        copy = hand_over(source, k, sems)
        copy.start()
        sent.append(copy)

    square = jnp.zeros((toks, 1), F32)
    for k in range(CHUNKS):
        for copy in act_copies[k]:
            copy.wait_recv()
        owner, number = origin(secs, sec, mb, act_pp, 0)
        piece = actrecv[k][owner, number].astype(F32)
        square = square + jnp.sum(piece * piece, axis=-1, keepdims=True)
        gath[k, me, :, pl.ds(0, kd)] = (piece * pre[:, k * kd:(k + 1) * kd]).astype(BF16)
        if k == CHUNKS - 1:
            root = jnp.broadcast_to(lax.rsqrt(square / d + 1e-06), (toks, LANES))
            high = root.astype(BF16).astype(F32)
            lane = lax.broadcasted_iota(jnp.int32, (toks, LANES), 1)
            gath[k, me, :, pl.ds(kd, LANES)] = jnp.where(
                lane == 0, high, jnp.where(lane == 1, root - high, 0.0)).astype(BF16)
        for way in range(2):
            copy = gather_copy(way, 1, k, me)
            copy.start()
            sent.append(copy)
        pass_on(me, k, own_sem.at[k])

    for name in ("acc", "blks", "loss"):
        loads[name].wait()
    term = jnp.full((brows, LANES), loss[0, 0], F32)
    high = term.astype(BF16).astype(F32)
    lane = lax.broadcasted_iota(jnp.int32, (brows, LANES), 1)
    row = lax.broadcasted_iota(jnp.int32, (brows, LANES), 0)
    tail = jnp.where(row > 0, 0.0, jnp.where(lane == 0, high, jnp.where(lane == 1, term - high, 0.0)))

    def pack(p, carry):
        for r in range(blk_pp):
            sacc[p, r, :, pl.ds(0, d)] = acc[pick(blks, me, n_dp, blk, p, r)].astype(BF16)
            sacc[p, r, :, pl.ds(d, LANES)] = tail.astype(BF16)
        return carry

    lax.fori_loop(0, n_dp, pack, 0)
    racc[me] = sacc[me]
    for j in range(mb):
        owner, number = origin(secs, sec, mb, act_pp, j)
        for k in range(CHUNKS):
            moved[j, :, k * kd:(k + 1) * kd] = actrecv[k][owner, number]

    def source_of(way, hop, c):
        return 2 * chip_at(pos - step_of[way] * hop) + c

    other = me + 1 - 2 * core

    def project(k):
        hand_over(other, k, own_sem.at[k]).wait_recv()
        for hop in range(1, far + 1):
            for way in range(2):
                if hop <= hops(way, k):
                    hand_over(source_of(way, hop, 1 - core), k, fwd_sem.at[way, hop - 1, k]).wait_recv()
        rows = gath[k, :, :, pl.ds(0, kd)].reshape(length, kd)
        terms = jnp.dot(rows, w[k * kd:(k + 1) * kd, :], preferred_element_type=F32)
        qkv[...] = terms if k == 0 else qkv[...] + terms

    for hop in range(1, far + 1):
        for k in range(CHUNKS):
            for way in range(2):
                if hop > hops(way, k):
                    continue
                source = source_of(way, hop, core)
                gather_copy(way, hop, k, source).wait_recv()
                if hop < hops(way, k):
                    copy = gather_copy(way, hop + 1, k, source)
                    copy.start()
                    sent.append(copy)
                pass_on(source, k, fwd_sem.at[way, hop - 1, k])
            if hop == far and k == 0:
                kv_copy.wait_recv()
                loads["wq"].wait()
            elif hop == far:
                project(k - 1)
        if hop == far - 1:
            blk_copies = []
            for o in range(1, n_dp):
                peer = (me + o) % n_dp
                copy = remote(sacc.at[peer], racc.at[me], blk_sem.at[o - 1], {"dp": peer})
                copy.start()
                blk_copies.append(copy)
    project(CHUNKS - 1)

    loads["rot"].wait()
    parts = gath[CHUNKS - 1, :, :, pl.ds(kd, LANES)].reshape(length, LANES).astype(F32)
    root = jnp.sum(parts, axis=-1, keepdims=True)
    cosine, sine = rot[0] * root, rot[1] * root

    def turned(v):
        return (v * cosine + pltpu.roll(v, hd // 2, 1) * sine).astype(BF16)

    queries = turned(qkv[:, 0:hd])
    keys = turned(qkv[:, hd:2 * hd])
    values = (qkv[:, 2 * hd:3 * hd] * root).astype(BF16)
    scores = lax.dot_general(queries, keys, (((1,), (1,)), ((), ())), preferred_element_type=F32)
    scores = scores * ((d / n_dp) ** (-0.5) / 50.0)
    at_query = lax.broadcasted_iota(jnp.int32, scores.shape, 0)
    at_key = lax.broadcasted_iota(jnp.int32, scores.shape, 1)
    expd = jnp.where(at_key <= at_query, jnp.exp(50.0 * jnp.tanh(scores)), 0.0)
    denominator = jnp.sum(expd, axis=-1, keepdims=True)
    numer = jnp.dot(expd.astype(BF16), values, preferred_element_type=F32)
    attended = (numer / denominator).astype(BF16)

    att[...] = attended.reshape(chips, 2, toks, hd)
    att_copy = remote(att.at[:, 1 - core], att_in, att_sem, partner)
    att_copy.start()
    wo_copy.wait_recv()
    ours = att[:, core].reshape(chips * toks, hd)
    att_copy.wait_recv()
    theirs = att_in[...].reshape(chips * toks, hd)
    even = core == 0
    both = jnp.concatenate([jnp.where(even, ours, theirs), jnp.where(even, theirs, ours)], axis=1)

    def ring_copy(way, step, k):
        return remote(ring_out.at[way, step - 1, k], ring_in.at[way, step - 1, k],
                      ring_sem.at[way, step - 1, k], device(pos + step_of[way]))

    for k in range(CHUNKS):
        terms = jnp.dot(both, wo[:, k * kd:(k + 1) * kd], preferred_element_type=F32)
        part[k] = terms.reshape(chips, toks, kd)
        for way in range(2):
            ring_out[way, 0, k] = part[k, chip_at(pos + step_of[way] * hops(way, k))].astype(BF16)
            copy = ring_copy(way, 1, k)
            copy.start()
            sent.append(copy)
    for step in range(1, far):
        for k in range(CHUNKS):
            for way in range(2):
                left = hops(way, k) - step
                if left < 1:
                    continue
                ring_copy(way, step, k).wait_recv()
                total = part[k, chip_at(pos + step_of[way] * left)] + ring_in[way, step - 1, k].astype(F32)
                ring_out[way, step, k] = total.astype(BF16)
                copy = ring_copy(way, step + 1, k)
                copy.start()
                sent.append(copy)

    for copy in blk_copies:
        copy.wait_recv()
    scale_sum = jnp.sum(racc[:, 0, :, pl.ds(d, LANES)].astype(F32), axis=0)
    factor = n_dp / jnp.sum(jnp.sum(scale_sum, axis=0, keepdims=True), axis=1, keepdims=True)

    def unpack(b, carry):
        owner, number = origin(blks, me, blk, blk_pp, b)
        accout[b] = racc[owner, number, :, pl.ds(0, d)].astype(F32) * factor
        return carry

    lax.fori_loop(0, blk, unpack, 0)

    pieces = []
    for k in range(CHUNKS):
        total = part[k, chip_at(pos)]
        for way in range(2):
            step = hops(way, k)
            ring_copy(way, step, k).wait_recv()
            total = total + ring_in[way, step - 1, k].astype(F32)
        pieces.append(total)
    loads["post"].wait()
    square = sum(jnp.sum(t * t, axis=-1, keepdims=True) for t in pieces)
    scale = lax.rsqrt(square / d + 1e-06)
    for k in range(CHUNKS):
        cols = slice(k * kd, (k + 1) * kd)
        outbuf[0, :, cols] = (
            moved[0, :, cols].astype(F32) + pieces[k] * scale * post[:, cols]
        ).astype(BF16)
    for copy in sum(act_copies, []) + [kv_copy, wo_copy, att_copy] + sent + blk_copies:
        copy.wait_send()


def write_out(moved, accout, outbuf, moved_hbm, newacc_hbm, check_hbm, sems):
    copies = [
        pltpu.make_async_copy(src, dst, sems.at[i])
        for i, (src, dst) in enumerate([(accout, newacc_hbm), (moved, moved_hbm), (outbuf, check_hbm)])
    ]
    for copy in copies:
        copy.start()
    for copy in copies:
        copy.wait()


def make_on_device(n_sec, n_dp):
    def on_device(activations, section_sources, accumulators, block_sources, loss_terms,
                  pre_gain, query_weight, keyval_weight, output_weight, post_gain):
        mb, toks, d = activations.shape
        blk, brows, _ = accumulators.shape
        hd = query_weight.shape[2]
        chips, far, kd, length = n_dp // 2, n_dp // 4, d // CHUNKS, n_dp * toks
        rot = jnp.asarray(rotary_tables(length, hd))
        smem = pltpu.SMEM
        in_hbm = pl.BlockSpec(memory_space=pltpu.HBM)
        vmem = pl.BlockSpec(memory_space=pltpu.VMEM)
        dma = pltpu.SemaphoreType.DMA
        act_pp, blk_pp = mb // n_sec, blk // n_dp
        out_bytes = activations.size * 2 + accumulators.size * 4 + toks * d * 2
        held = pl.pallas_call(
            functools.partial(kernel, (n_sec, n_dp)),
            out_shape=(
                pltpu.VMEM(activations.shape, BF16),
                pltpu.VMEM(accumulators.shape, F32),
                pltpu.VMEM((1, toks, d), BF16),
            ),
            in_specs=[in_hbm] * 11,
            out_specs=(vmem,) * 3,
            scratch_shapes=[
                smem(section_sources.shape, jnp.int32),
                smem(block_sources.shape, jnp.int32),
                smem((1, 1), F32),
                pltpu.VMEM(activations.shape, BF16),
                pltpu.VMEM(accumulators.shape, F32),
                pltpu.VMEM((1, d), F32),
                pltpu.VMEM((1, d), F32),
                pltpu.VMEM(rot.shape, F32),
                pltpu.VMEM((d, 3 * hd), BF16),
                pltpu.VMEM((2 * hd, d), BF16),
                pltpu.VMEM((n_sec, CHUNKS, act_pp, toks, kd), BF16),
                (pltpu.VMEM((n_sec, act_pp, toks, kd), BF16),) * CHUNKS,
                pltpu.VMEM((n_dp, blk_pp, brows, d + LANES), BF16),
                pltpu.VMEM((n_dp, blk_pp, brows, d + LANES), BF16),
                pltpu.VMEM((CHUNKS, n_dp, toks, kd + LANES), BF16),
                pltpu.VMEM((length, 3 * hd), F32),
                pltpu.VMEM((chips, 2, toks, hd), BF16),
                pltpu.VMEM((chips, toks, hd), BF16),
                pltpu.VMEM((CHUNKS, chips, toks, kd), F32),
                pltpu.VMEM((2, far, CHUNKS, toks, kd), BF16),
                pltpu.VMEM((2, far, CHUNKS, toks, kd), BF16),
                dma((11,)),
                dma((n_sec - 1, CHUNKS, 2)),
                dma((2,)),
                dma((2,)),
                dma((n_dp - 1, 2)),
                dma((2, far, CHUNKS, 2)),
                dma((CHUNKS, 2)),
                dma((2, far, CHUNKS, 2)),
                dma((2,)),
                dma((2, far, CHUNKS, 2)),
            ],
            compiler_params=pltpu.CompilerParams(
                collective_id=0, has_side_effects=True, vmem_limit_bytes=VMEM_BYTES - 2**16 - out_bytes
            ),
        )(section_sources, block_sources, loss_terms, activations, accumulators,
          pre_gain, query_weight, keyval_weight, output_weight, post_gain, rot)
        return pl.pallas_call(
            write_out,
            out_shape=(
                jax.ShapeDtypeStruct(activations.shape, BF16),
                jax.ShapeDtypeStruct(accumulators.shape, F32),
                jax.ShapeDtypeStruct((1, toks, d), BF16),
            ),
            in_specs=[vmem] * 3,
            out_specs=(in_hbm,) * 3,
            scratch_shapes=[dma((3,))],
            compiler_params=pltpu.CompilerParams(vmem_limit_bytes=4 * 2**20),
        )(*held)

    return on_device


def solution(mesh):
    placed = (
        P("section", "dp", None),
        P(),
        P("dp", "section", None),
        P(),
        P("section", "dp"),
        P("section", None),
        P("section", None, "dp"),
        P("section", None, "dp"),
        P("section", "dp", None),
        P("section", None),
    )
    return jax.shard_map(
        make_on_device(mesh.shape["section"], mesh.shape["dp"]),
        mesh=mesh,
        in_specs=placed,
        out_specs=(P("section", "dp", None), P("dp", "section", None), P("section", "dp", None)),
        check_vma=False,
    )
```

time: 61.9 us -> 51.7 us (0.84)
  local copies, waits for them, and re-layouts: 6.91 us -> 0 us
  Pallas kernels: 52.1 us -> 50.2 us
  other arithmetic: 1.27 us -> 0 us
    unnamed x5 -> x0, local copies, waits for them, and re-layouts: 4.31 us -> none
    pallas_call x1 -> x2, Pallas kernels: 52.1 us -> 50.2 us  [the longest x1 49.2 us: on_device(): pl.pallas_call(functools.partial(kernel, (n_sec, n_dp)), out_shape=(pltpu...]
    reshape x2 -> x0, local copies, waits for them, and re-layouts: 1.49 us -> none  [routes(): table = sources.reshape(groups, per_group)]
    squeeze x2 -> x0, local copies, waits for them, and re-layouts: 1.11 us -> none  [routes(): my_owners = lax.dynamic_slice_in_dim(owners, own, 1, 0)[0]]
    select_n x1 -> x0, other arithmetic: 0.64 us -> none  [routes(): owners = table // per_group]
    reduce_sum x1 -> x0, other arithmetic: 0.64 us -> none  [routes(): send = jnp.sum(jnp.where(mine, places, 0), axis=1)]
where the time goes in v2:
time: 51.7 us; the launch traced here: 51.5 us
  Pallas kernels  50.2 us (97%)
  between operations  1.29 us (2%)
    pallas_call x1, Pallas kernels, on_device(): pl.pallas_call(functools.partial(kernel, (n_sec, n_dp)), out_shape=(pltpu...  49.2 us

profile of v2, /device:TPU:0, one launch (start us, length us, event | category | flops | bytes accessed | tf_op | source)
XLA Modules:
  0.0 51.5 jit_solution(2255192236021398551)
XLA Ops:
  1.3 49.2 %shard_map.130 = (bf16[2,16,4608]{2,1,0:T(8,128)(2,1)S(1)}, f32[16,2,4608]{2,1,0:T(2,128)S(1)}, bf16[1,16,4608]{2,1,0:T(8,128)(2,1)S(1)}) custom-call(s32[4]{0:T(128)} %secs_hbm.1, s32[256]{0:T(256)} %blks_hbm.1, f32[1,1]{1,0:T(1,128)S(6)} %copy.14.loss_hbm, bf16[2,16,4608]{2,1,0:T(8,128)(2,1)} %act_hbm.1, f32[16,2,4608]{2,1,0:T(2,128)} %acc_hbm.1, ...), custom_call_target="tpu_custom_call" | custom-call | tf_op jit(solution)/shard_map/pallas_call | solution.py:360
  50.5 1.0 %shard_map.131 = (bf16[2,16,4608]{2,1,0:T(8,128)(2,1)}, f32[16,2,4608]{2,1,0:T(2,128)}, bf16[1,16,4608]{2,1,0:T(8,128)(2,1)}) custom-call(bf16[2,16,4608]{2,1,0:T(8,128)(2,1)S(1)} %get-tuple-element.6.moved, f32[16,2,4608]{2,1,0:T(2,128)S(1)} %get-tuple-element.7.accout, bf16[1,16,4608]{2,1,0:T(8,128)(2,1)S(1)} %get-tuple-element.8.outbuf), custom_call_target="tpu_custom_call" | custom-call | tf_op jit(solution)/shard_map/pallas_call | solution.py:407

commit v3 on v2

--- a/solution.py
+++ b/solution.py
@@ -10,7 +10,7 @@
 
 LANES = 128
 VMEM_BYTES = 67043328
-CHUNKS = 4
+CHUNKS = 6
 F32 = jnp.float32
 BF16 = jnp.bfloat16
 
@@ -92,9 +92,8 @@
     for o in range(1, n_sec):
         pl.semaphore_signal(barrier, inc=1, device_id={"section": (sec + o) % n_sec},
                             device_id_type=pl.DeviceIdType.MESH)
-    for o in range(1, n_dp):
-        pl.semaphore_signal(barrier, inc=1, device_id={"dp": (me + o) % n_dp},
-                            device_id_type=pl.DeviceIdType.MESH)
+    for near in (device(pos + 1), device(pos - 1), partner):
+        pl.semaphore_signal(barrier, inc=1, device_id=near, device_id_type=pl.DeviceIdType.MESH)
 
     kv_cols = pl.ds(pl.multiple_of(hd + core * hd, LANES), hd)
     q_cols = pl.ds(0, hd)
@@ -119,7 +118,7 @@
             block = act[pick(secs, sec, n_sec, mb, q, r)]
             for k in range(CHUNKS):
                 stage[q, k, r] = block[:, k * kd:(k + 1) * kd]
-    pl.semaphore_wait(barrier, n_sec - 1 + n_dp - 1)
+    pl.semaphore_wait(barrier, n_sec - 1 + 3)
     act_copies = [[] for _ in range(CHUNKS)]
     for k in range(CHUNKS):
         for o in range(1, n_sec):
@@ -137,6 +136,23 @@
     wo_copy = remote(wo.at[wo_rows], wo.at[wo_rows], wo_sem, partner)
     wo_copy.start()
     loads["pre"].wait()
+
+    for name in ("acc", "blks", "loss"):
+        loads[name].wait()
+    term = jnp.full((brows, LANES), loss[0, 0], F32)
+    high = term.astype(BF16).astype(F32)
+    lane = lax.broadcasted_iota(jnp.int32, (brows, LANES), 1)
+    row = lax.broadcasted_iota(jnp.int32, (brows, LANES), 0)
+    tail = jnp.where(row > 0, 0.0, jnp.where(lane == 0, high, jnp.where(lane == 1, term - high, 0.0)))
+
+    def pack(p, carry):
+        for r in range(blk_pp):
+            sacc[p, r, :, pl.ds(0, d)] = acc[pick(blks, me, n_dp, blk, p, r)].astype(BF16)
+            sacc[p, r, :, pl.ds(d, LANES)] = tail.astype(BF16)
+        return carry
+
+    lax.fori_loop(0, n_dp, pack, 0)
+    racc[me] = sacc[me]
 
     def hops(way, k):
         return far if (k < CHUNKS // 2) == (way == 0) else far - 1
@@ -183,27 +199,6 @@
             sent.append(copy)
         pass_on(me, k, own_sem.at[k])
 
-    for name in ("acc", "blks", "loss"):
-        loads[name].wait()
-    term = jnp.full((brows, LANES), loss[0, 0], F32)
-    high = term.astype(BF16).astype(F32)
-    lane = lax.broadcasted_iota(jnp.int32, (brows, LANES), 1)
-    row = lax.broadcasted_iota(jnp.int32, (brows, LANES), 0)
-    tail = jnp.where(row > 0, 0.0, jnp.where(lane == 0, high, jnp.where(lane == 1, term - high, 0.0)))
-
-    def pack(p, carry):
-        for r in range(blk_pp):
-            sacc[p, r, :, pl.ds(0, d)] = acc[pick(blks, me, n_dp, blk, p, r)].astype(BF16)
-            sacc[p, r, :, pl.ds(d, LANES)] = tail.astype(BF16)
-        return carry
-
-    lax.fori_loop(0, n_dp, pack, 0)
-    racc[me] = sacc[me]
-    for j in range(mb):
-        owner, number = origin(secs, sec, mb, act_pp, j)
-        for k in range(CHUNKS):
-            moved[j, :, k * kd:(k + 1) * kd] = actrecv[k][owner, number]
-
     def source_of(way, hop, c):
         return 2 * chip_at(pos - step_of[way] * hop) + c
 
@@ -219,6 +214,20 @@
         terms = jnp.dot(rows, w[k * kd:(k + 1) * kd, :], preferred_element_type=F32)
         qkv[...] = terms if k == 0 else qkv[...] + terms
 
+    blk_copies = []
+
+    def send_block(peer, slot):
+        copy = remote(sacc.at[peer], racc.at[me], blk_sem.at[slot], {"dp": peer})
+        copy.start()
+        blk_copies.append(copy)
+
+    def send_blocks(places):
+        for way, hop in places:
+            for c in range(2):
+                peer = 2 * chip_at(pos + step_of[way] * hop) + (core + c) % 2
+                send_block(peer, 1 + (way * far + hop - 1) * 2 + c)
+
+    send_block(other, 0)
     for hop in range(1, far + 1):
         for k in range(CHUNKS):
             for way in range(2):
@@ -237,12 +246,8 @@
             elif hop == far:
                 project(k - 1)
         if hop == far - 1:
-            blk_copies = []
-            for o in range(1, n_dp):
-                peer = (me + o) % n_dp
-                copy = remote(sacc.at[peer], racc.at[me], blk_sem.at[o - 1], {"dp": peer})
-                copy.start()
-                blk_copies.append(copy)
+            send_blocks([(way, h) for h in range(1, far) for way in range(2)])
+    send_blocks([(0, far)])
     project(CHUNKS - 1)
 
     loads["rot"].wait()
@@ -287,6 +292,23 @@
             copy = ring_copy(way, 1, k)
             copy.start()
             sent.append(copy)
+    for j in range(mb):
+        owner, number = origin(secs, sec, mb, act_pp, j)
+        for k in range(CHUNKS):
+            moved[j, :, k * kd:(k + 1) * kd] = actrecv[k][owner, number]
+
+    for copy in blk_copies:
+        copy.wait_recv()
+    scale_sum = jnp.sum(racc[:, 0, :, pl.ds(d, LANES)].astype(F32), axis=0)
+    factor = n_dp / jnp.sum(jnp.sum(scale_sum, axis=0, keepdims=True), axis=1, keepdims=True)
+
+    def unpack(b, carry):
+        owner, number = origin(blks, me, blk, blk_pp, b)
+        accout[b] = racc[owner, number, :, pl.ds(0, d)].astype(F32) * factor
+        return carry
+
+    lax.fori_loop(0, blk, unpack, 0)
+
     for step in range(1, far):
         for k in range(CHUNKS):
             for way in range(2):
@@ -299,18 +321,6 @@
                 copy = ring_copy(way, step + 1, k)
                 copy.start()
                 sent.append(copy)
-
-    for copy in blk_copies:
-        copy.wait_recv()
-    scale_sum = jnp.sum(racc[:, 0, :, pl.ds(d, LANES)].astype(F32), axis=0)
-    factor = n_dp / jnp.sum(jnp.sum(scale_sum, axis=0, keepdims=True), axis=1, keepdims=True)
-
-    def unpack(b, carry):
-        owner, number = origin(blks, me, blk, blk_pp, b)
-        accout[b] = racc[owner, number, :, pl.ds(0, d)].astype(F32) * factor
-        return carry
-
-    lax.fori_loop(0, blk, unpack, 0)
 
     pieces = []
     for k in range(CHUNKS):
@@ -392,7 +402,7 @@
                 dma((n_sec - 1, CHUNKS, 2)),
                 dma((2,)),
                 dma((2,)),
-                dma((n_dp - 1, 2)),
+                dma((1 + 4 * far, 2)),
                 dma((2, far, CHUNKS, 2)),
                 dma((CHUNKS, 2)),
                 dma((2, far, CHUNKS, 2)),

time: 51.7 us -> 47.5 us (0.919)
  Pallas kernels: 50.2 us -> 46.1 us
    pallas_call x1, Pallas kernels: 49.2 us -> 45.1 us  [on_device(): pl.pallas_call(functools.partial(kernel, (n_sec, n_dp)), out_shape=(pltpu...]
where the time goes in v3:
time: 47.5 us; the launch traced here: 47.3 us
  Pallas kernels  46.1 us (97%)
  between operations  1.29 us (3%)
    pallas_call x1, Pallas kernels, on_device(): pl.pallas_call(functools.partial(kernel, (n_sec, n_dp)), out_shape=(pltpu...  45.1 us
    pallas_call x1, Pallas kernels, on_device(): pl.pallas_call(write_out, out_shape=(jax.ShapeDtypeStruct(activations.sha...  0.98 us

profile of v3, /device:TPU:0, one launch (start us, length us, event | category | flops | bytes accessed | tf_op | source)
XLA Modules:
  0.0 47.3 jit_solution(13763242922968911224)
XLA Ops:
  1.3 45.1 %shard_map.130 = (bf16[2,16,4608]{2,1,0:T(8,128)(2,1)S(1)}, f32[16,2,4608]{2,1,0:T(2,128)S(1)}, bf16[1,16,4608]{2,1,0:T(8,128)(2,1)S(1)}) custom-call(s32[4]{0:T(128)} %secs_hbm.1, s32[256]{0:T(256)} %blks_hbm.1, f32[1,1]{1,0:T(1,128)S(6)} %copy.14.loss_hbm, bf16[2,16,4608]{2,1,0:T(8,128)(2,1)} %act_hbm.1, f32[16,2,4608]{2,1,0:T(2,128)} %acc_hbm.1, ...), custom_call_target="tpu_custom_call" | custom-call | tf_op jit(solution)/shard_map/pallas_call | solution.py:370
  46.4 1.0 %shard_map.131 = (bf16[2,16,4608]{2,1,0:T(8,128)(2,1)}, f32[16,2,4608]{2,1,0:T(2,128)}, bf16[1,16,4608]{2,1,0:T(8,128)(2,1)}) custom-call(bf16[2,16,4608]{2,1,0:T(8,128)(2,1)S(1)} %get-tuple-element.6.moved, f32[16,2,4608]{2,1,0:T(2,128)S(1)} %get-tuple-element.7.accout, bf16[1,16,4608]{2,1,0:T(8,128)(2,1)S(1)} %get-tuple-element.8.outbuf), custom_call_target="tpu_custom_call" | custom-call | tf_op jit(solution)/shard_map/pallas_call | solution.py:417

commit v4 on v3

--- a/solution.py
+++ b/solution.py
@@ -56,7 +56,7 @@
     secs, blks, loss, act, acc, pre, post, rot, w, wo,
     stage, actrecv, sacc, racc,
     gath, qkv, att, att_in, part, ring_in, ring_out,
-    load_sem, act_sem, w_sem, wo_sem, blk_sem, ag_sem, own_sem, fwd_sem, att_sem, ring_sem,
+    load_sem, act_out, act_sem, w_sem, wo_sem, blk_sem, ag_out, ag_sem, fwd_sem, att_sem, ring_done, ring_sem,
 ):
     n_sec, n_dp = dims
     mb, toks, d = act.shape
@@ -82,9 +82,9 @@
 
     partner = {"dp": me + 1 - 2 * core}
 
-    def remote(src, dst, sems, dev):
+    def remote(src, dst, send_sem, recv_sem, dev):
         return pltpu.make_async_remote_copy(
-            src_ref=src, dst_ref=dst, send_sem=sems.at[0], recv_sem=sems.at[1],
+            src_ref=src, dst_ref=dst, send_sem=send_sem, recv_sem=recv_sem,
             device_id=dev, device_id_type=pl.DeviceIdType.MESH,
         )
 
@@ -123,17 +123,17 @@
     for k in range(CHUNKS):
         for o in range(1, n_sec):
             q = (sec + o) % n_sec
-            copy = remote(stage.at[q, k], actrecv[k].at[sec], act_sem.at[o - 1, k], {"section": q})
+            copy = remote(stage.at[q, k], actrecv[k].at[sec], act_out.at[o - 1], act_sem.at[o - 1, k], {"section": q})
             copy.start()
             act_copies[k].append(copy)
     for k in range(CHUNKS):
         actrecv[k][sec] = stage[sec, k]
 
     loads["wkv"].wait()
-    kv_copy = remote(w.at[:, kv_cols], w.at[:, kv_cols], w_sem, partner)
+    kv_copy = remote(w.at[:, kv_cols], w.at[:, kv_cols], w_sem.at[0], w_sem.at[1], partner)
     kv_copy.start()
     loads["wo"].wait()
-    wo_copy = remote(wo.at[wo_rows], wo.at[wo_rows], wo_sem, partner)
+    wo_copy = remote(wo.at[wo_rows], wo.at[wo_rows], wo_sem.at[0], wo_sem.at[1], partner)
     wo_copy.start()
     loads["pre"].wait()
 
@@ -158,26 +158,20 @@
         return far if (k < CHUNKS // 2) == (way == 0) else far - 1
 
     step_of = (1, -1)
-    sent = []
 
     def width(k):
         return kd + LANES if k == CHUNKS - 1 else kd
 
-    def block_of(k, source):
-        return gath.at[k, source, :, pl.ds(0, width(k))]
-
-    def gather_copy(way, hop, k, source):
-        block = block_of(k, source)
-        return remote(block, block, ag_sem.at[way, hop - 1, k], device(pos + step_of[way]))
-
-    def hand_over(source, k, sems):
-        block = block_of(k, source)
-        return remote(block, block, sems, partner)
-
-    def pass_on(source, k, sems):
-        copy = hand_over(source, k, sems)
-        copy.start()
-        sent.append(copy)
+    def blocks_of(k, c, places):
+        return gath.at[k, c, places, :, pl.ds(0, width(k))]
+
+    def gather_copy(way, hop, k, place):
+        block = blocks_of(k, core, place)
+        return remote(block, block, ag_out.at[k], ag_sem.at[way, hop - 1, k], device(pos + step_of[way]))
+
+    def pass_on(place, k):
+        block = blocks_of(k, core, place)
+        remote(block, block, fwd_sem.at[0, k], fwd_sem.at[1, k], partner).start()
 
     square = jnp.zeros((toks, 1), F32)
     for k in range(CHUNKS):
@@ -186,60 +180,45 @@
         owner, number = origin(secs, sec, mb, act_pp, 0)
         piece = actrecv[k][owner, number].astype(F32)
         square = square + jnp.sum(piece * piece, axis=-1, keepdims=True)
-        gath[k, me, :, pl.ds(0, kd)] = (piece * pre[:, k * kd:(k + 1) * kd]).astype(BF16)
+        gath[k, core, chip, :, pl.ds(0, kd)] = (piece * pre[:, k * kd:(k + 1) * kd]).astype(BF16)
         if k == CHUNKS - 1:
             root = jnp.broadcast_to(lax.rsqrt(square / d + 1e-06), (toks, LANES))
             high = root.astype(BF16).astype(F32)
             lane = lax.broadcasted_iota(jnp.int32, (toks, LANES), 1)
-            gath[k, me, :, pl.ds(kd, LANES)] = jnp.where(
+            gath[k, core, chip, :, pl.ds(kd, LANES)] = jnp.where(
                 lane == 0, high, jnp.where(lane == 1, root - high, 0.0)).astype(BF16)
         for way in range(2):
-            copy = gather_copy(way, 1, k, me)
-            copy.start()
-            sent.append(copy)
-        pass_on(me, k, own_sem.at[k])
-
-    def source_of(way, hop, c):
-        return 2 * chip_at(pos - step_of[way] * hop) + c
+            gather_copy(way, 1, k, chip).start()
+        pass_on(chip, k)
 
     other = me + 1 - 2 * core
 
     def project(k):
-        hand_over(other, k, own_sem.at[k]).wait_recv()
-        for hop in range(1, far + 1):
-            for way in range(2):
-                if hop <= hops(way, k):
-                    hand_over(source_of(way, hop, 1 - core), k, fwd_sem.at[way, hop - 1, k]).wait_recv()
-        rows = gath[k, :, :, pl.ds(0, kd)].reshape(length, kd)
+        block = blocks_of(k, 1 - core, slice(None))
+        remote(block, block, fwd_sem.at[0, k], fwd_sem.at[1, k], partner).wait_recv()
+        rows = gath[k, :, :, :, pl.ds(0, kd)].reshape(length, kd)
         terms = jnp.dot(rows, w[k * kd:(k + 1) * kd, :], preferred_element_type=F32)
         qkv[...] = terms if k == 0 else qkv[...] + terms
 
-    blk_copies = []
-
-    def send_block(peer, slot):
-        copy = remote(sacc.at[peer], racc.at[me], blk_sem.at[slot], {"dp": peer})
-        copy.start()
-        blk_copies.append(copy)
+    def send_block(peer):
+        remote(sacc.at[peer], racc.at[me], blk_sem.at[0], blk_sem.at[1], {"dp": peer}).start()
 
     def send_blocks(places):
         for way, hop in places:
             for c in range(2):
-                peer = 2 * chip_at(pos + step_of[way] * hop) + (core + c) % 2
-                send_block(peer, 1 + (way * far + hop - 1) * 2 + c)
-
-    send_block(other, 0)
+                send_block(2 * chip_at(pos + step_of[way] * hop) + (core + c) % 2)
+
+    send_block(other)
     for hop in range(1, far + 1):
         for k in range(CHUNKS):
             for way in range(2):
                 if hop > hops(way, k):
                     continue
-                source = source_of(way, hop, core)
-                gather_copy(way, hop, k, source).wait_recv()
+                place = chip_at(pos - step_of[way] * hop)
+                gather_copy(way, hop, k, place).wait_recv()
                 if hop < hops(way, k):
-                    copy = gather_copy(way, hop + 1, k, source)
-                    copy.start()
-                    sent.append(copy)
-                pass_on(source, k, fwd_sem.at[way, hop - 1, k])
+                    gather_copy(way, hop + 1, k, place).start()
+                pass_on(place, k)
             if hop == far and k == 0:
                 kv_copy.wait_recv()
                 loads["wq"].wait()
@@ -251,54 +230,56 @@
     project(CHUNKS - 1)
 
     loads["rot"].wait()
-    parts = gath[CHUNKS - 1, :, :, pl.ds(kd, LANES)].reshape(length, LANES).astype(F32)
+    parts = gath[CHUNKS - 1, :, :, :, pl.ds(kd, LANES)].reshape(length, LANES).astype(F32)
     root = jnp.sum(parts, axis=-1, keepdims=True)
     cosine, sine = rot[0] * root, rot[1] * root
 
     def turned(v):
         return (v * cosine + pltpu.roll(v, hd // 2, 1) * sine).astype(BF16)
+
+    def token_at(shape, dim):
+        row = lax.broadcasted_iota(jnp.int32, shape, dim)
+        block = row // toks
+        return (block % chips * 2 + block // chips) * toks + row % toks
 
     queries = turned(qkv[:, 0:hd])
     keys = turned(qkv[:, hd:2 * hd])
     values = (qkv[:, 2 * hd:3 * hd] * root).astype(BF16)
     scores = lax.dot_general(queries, keys, (((1,), (1,)), ((), ())), preferred_element_type=F32)
     scores = scores * ((d / n_dp) ** (-0.5) / 50.0)
-    at_query = lax.broadcasted_iota(jnp.int32, scores.shape, 0)
-    at_key = lax.broadcasted_iota(jnp.int32, scores.shape, 1)
-    expd = jnp.where(at_key <= at_query, jnp.exp(50.0 * jnp.tanh(scores)), 0.0)
+    expd = jnp.where(token_at((1, length), 1) <= token_at((length, 1), 0), jnp.exp(50.0 * jnp.tanh(scores)), 0.0)
     denominator = jnp.sum(expd, axis=-1, keepdims=True)
     numer = jnp.dot(expd.astype(BF16), values, preferred_element_type=F32)
     attended = (numer / denominator).astype(BF16)
 
-    att[...] = attended.reshape(chips, 2, toks, hd)
-    att_copy = remote(att.at[:, 1 - core], att_in, att_sem, partner)
+    att[...] = attended.reshape(2, chips, toks, hd)
+    att_copy = remote(att.at[1 - core], att_in, att_sem.at[0], att_sem.at[1], partner)
     att_copy.start()
     wo_copy.wait_recv()
-    ours = att[:, core].reshape(chips * toks, hd)
+    ours = att[core].reshape(chips * toks, hd)
     att_copy.wait_recv()
     theirs = att_in[...].reshape(chips * toks, hd)
     even = core == 0
     both = jnp.concatenate([jnp.where(even, ours, theirs), jnp.where(even, theirs, ours)], axis=1)
 
     def ring_copy(way, step, k):
-        return remote(ring_out.at[way, step - 1, k], ring_in.at[way, step - 1, k],
-                      ring_sem.at[way, step - 1, k], device(pos + step_of[way]))
+        return remote(ring_out.at[k, way * far + step - 1], ring_in.at[k, way * far + step - 1],
+                      ring_done.at[k], ring_sem.at[way, step - 1, k], device(pos + step_of[way]))
 
     for k in range(CHUNKS):
         terms = jnp.dot(both, wo[:, k * kd:(k + 1) * kd], preferred_element_type=F32)
         part[k] = terms.reshape(chips, toks, kd)
         for way in range(2):
-            ring_out[way, 0, k] = part[k, chip_at(pos + step_of[way] * hops(way, k))].astype(BF16)
-            copy = ring_copy(way, 1, k)
-            copy.start()
-            sent.append(copy)
+            ring_out[k, way * far] = part[k, chip_at(pos + step_of[way] * hops(way, k))].astype(BF16)
+            ring_copy(way, 1, k).start()
     for j in range(mb):
         owner, number = origin(secs, sec, mb, act_pp, j)
         for k in range(CHUNKS):
             moved[j, :, k * kd:(k + 1) * kd] = actrecv[k][owner, number]
 
-    for copy in blk_copies:
-        copy.wait_recv()
+    others = pl.ds(0, n_dp - 1)
+    all_blocks = remote(sacc.at[others], racc.at[others], blk_sem.at[0], blk_sem.at[1], partner)
+    all_blocks.wait_recv()
     scale_sum = jnp.sum(racc[:, 0, :, pl.ds(d, LANES)].astype(F32), axis=0)
     factor = n_dp / jnp.sum(jnp.sum(scale_sum, axis=0, keepdims=True), axis=1, keepdims=True)
 
@@ -316,11 +297,9 @@
                 if left < 1:
                     continue
                 ring_copy(way, step, k).wait_recv()
-                total = part[k, chip_at(pos + step_of[way] * left)] + ring_in[way, step - 1, k].astype(F32)
-                ring_out[way, step, k] = total.astype(BF16)
-                copy = ring_copy(way, step + 1, k)
-                copy.start()
-                sent.append(copy)
+                total = part[k, chip_at(pos + step_of[way] * left)] + ring_in[k, way * far + step - 1].astype(F32)
+                ring_out[k, way * far + step] = total.astype(BF16)
+                ring_copy(way, step + 1, k).start()
 
     pieces = []
     for k in range(CHUNKS):
@@ -328,7 +307,7 @@
         for way in range(2):
             step = hops(way, k)
             ring_copy(way, step, k).wait_recv()
-            total = total + ring_in[way, step - 1, k].astype(F32)
+            total = total + ring_in[k, way * far + step - 1].astype(F32)
         pieces.append(total)
     loads["post"].wait()
     square = sum(jnp.sum(t * t, axis=-1, keepdims=True) for t in pieces)
@@ -338,8 +317,17 @@
         outbuf[0, :, cols] = (
             moved[0, :, cols].astype(F32) + pieces[k] * scale * post[:, cols]
         ).astype(BF16)
-    for copy in sum(act_copies, []) + [kv_copy, wo_copy, att_copy] + sent + blk_copies:
+    for copy in (kv_copy, wo_copy, att_copy, all_blocks):
         copy.wait_send()
+    for o in range(1, n_sec):
+        q = (sec + o) % n_sec
+        remote(stage.at[q], stage.at[q], act_out.at[o - 1], act_sem.at[o - 1, 0], {"section": q}).wait_send()
+    for k in range(CHUNKS):
+        for places, sem in ((slice(None), fwd_sem.at[0, k]), (pl.ds(0, chips - 1), ag_out.at[k])):
+            block = blocks_of(k, core, places)
+            remote(block, block, sem, fwd_sem.at[1, k], partner).wait_send()
+        block = ring_out.at[k, pl.ds(0, chips - 1)]
+        remote(block, block, ring_done.at[k], fwd_sem.at[1, k], partner).wait_send()
 
 
 def write_out(moved, accout, outbuf, moved_hbm, newacc_hbm, check_hbm, sems):
@@ -360,7 +348,8 @@
         blk, brows, _ = accumulators.shape
         hd = query_weight.shape[2]
         chips, far, kd, length = n_dp // 2, n_dp // 4, d // CHUNKS, n_dp * toks
-        rot = jnp.asarray(rotary_tables(length, hd))
+        order = np.arange(length).reshape(chips, 2, toks).transpose(1, 0, 2).reshape(-1)
+        rot = jnp.asarray(rotary_tables(length, hd)[:, order])
         smem = pltpu.SMEM
         in_hbm = pl.BlockSpec(memory_space=pltpu.HBM)
         vmem = pl.BlockSpec(memory_space=pltpu.VMEM)
@@ -391,23 +380,25 @@
                 (pltpu.VMEM((n_sec, act_pp, toks, kd), BF16),) * CHUNKS,
                 pltpu.VMEM((n_dp, blk_pp, brows, d + LANES), BF16),
                 pltpu.VMEM((n_dp, blk_pp, brows, d + LANES), BF16),
-                pltpu.VMEM((CHUNKS, n_dp, toks, kd + LANES), BF16),
+                pltpu.VMEM((CHUNKS, 2, chips, toks, kd + LANES), BF16),
                 pltpu.VMEM((length, 3 * hd), F32),
-                pltpu.VMEM((chips, 2, toks, hd), BF16),
+                pltpu.VMEM((2, chips, toks, hd), BF16),
                 pltpu.VMEM((chips, toks, hd), BF16),
                 pltpu.VMEM((CHUNKS, chips, toks, kd), F32),
-                pltpu.VMEM((2, far, CHUNKS, toks, kd), BF16),
-                pltpu.VMEM((2, far, CHUNKS, toks, kd), BF16),
+                pltpu.VMEM((CHUNKS, 2 * far, toks, kd), BF16),
+                pltpu.VMEM((CHUNKS, 2 * far, toks, kd), BF16),
                 dma((11,)),
-                dma((n_sec - 1, CHUNKS, 2)),
+                dma((n_sec - 1,)),
+                dma((n_sec - 1, CHUNKS)),
                 dma((2,)),
                 dma((2,)),
-                dma((1 + 4 * far, 2)),
-                dma((2, far, CHUNKS, 2)),
-                dma((CHUNKS, 2)),
-                dma((2, far, CHUNKS, 2)),
                 dma((2,)),
-                dma((2, far, CHUNKS, 2)),
+                dma((CHUNKS,)),
+                dma((2, far, CHUNKS)),
+                dma((2, CHUNKS)),
+                dma((2,)),
+                dma((CHUNKS,)),
+                dma((2, far, CHUNKS)),
             ],
             compiler_params=pltpu.CompilerParams(
                 collective_id=0, has_side_effects=True, vmem_limit_bytes=VMEM_BYTES - 2**16 - out_bytes

time: 47.5 us -> 45.4 us (0.956)
  Pallas kernels: 46.1 us -> 43.9 us
    pallas_call x1, Pallas kernels: 45.1 us -> 42.9 us  [on_device(): pl.pallas_call(functools.partial(kernel, (n_sec, n_dp)), out_shape=(pltpu...]
where the time goes in v4:
time: 45.4 us; the launch traced here: 45.2 us
  Pallas kernels  43.9 us (97%)
  between operations  1.29 us (3%)
    pallas_call x1, Pallas kernels, on_device(): pl.pallas_call(functools.partial(kernel, (n_sec, n_dp)), out_shape=(pltpu...  42.9 us
    pallas_call x1, Pallas kernels, on_device(): pl.pallas_call(write_out, out_shape=(jax.ShapeDtypeStruct(activations.sha...  0.98 us

profile of v4, /device:TPU:0, one launch (start us, length us, event | category | flops | bytes accessed | tf_op | source)
XLA Modules:
  0.0 45.2 jit_solution(10466330747779057398)
XLA Ops:
  1.3 42.9 %shard_map.130 = (bf16[2,16,4608]{2,1,0:T(8,128)(2,1)S(1)}, f32[16,2,4608]{2,1,0:T(2,128)S(1)}, bf16[1,16,4608]{2,1,0:T(8,128)(2,1)S(1)}) custom-call(s32[4]{0:T(128)} %secs_hbm.1, s32[256]{0:T(256)} %blks_hbm.1, f32[1,1]{1,0:T(1,128)S(6)} %copy.14.loss_hbm, bf16[2,16,4608]{2,1,0:T(8,128)(2,1)} %act_hbm.1, f32[16,2,4608]{2,1,0:T(2,128)} %acc_hbm.1, ...), custom_call_target="tpu_custom_call" | custom-call | tf_op jit(solution)/shard_map/pallas_call | solution.py:359
  44.2 1.0 %shard_map.131 = (bf16[2,16,4608]{2,1,0:T(8,128)(2,1)}, f32[16,2,4608]{2,1,0:T(2,128)}, bf16[1,16,4608]{2,1,0:T(8,128)(2,1)}) custom-call(bf16[2,16,4608]{2,1,0:T(8,128)(2,1)S(1)} %get-tuple-element.6.moved, f32[16,2,4608]{2,1,0:T(2,128)S(1)} %get-tuple-element.7.accout, bf16[1,16,4608]{2,1,0:T(8,128)(2,1)S(1)} %get-tuple-element.8.outbuf), custom_call_target="tpu_custom_call" | custom-call | tf_op jit(solution)/shard_map/pallas_call | solution.py:408
